TPU v7x, 32 devices: a whole 2x2x4 slice. The times are simulated.
32 devices in a mesh: gx: 4 (over y, core), gy: 8 (over z, x).
Axes of the slice: x: 2, y: 2, z: 4, core: 2. Of those that a mesh axis runs over, the one named last changes fastest.
Arguments:
- transfer: bfloat16 [512, 75, 128], P(('gx', 'gy')), may hold values from -6 to 6
- positions: float32 [512, 3, 128], P(('gx', 'gy')), may hold values from -4 to 4
- normals: float32 [512, 3, 128], P(('gx', 'gy')), may hold values from -4 to 4
- area: float32 [512, 128], P(('gx', 'gy')), may hold values from 0.06 to 3
- albedo: float32 [512, 3, 128], P(('gx', 'gy')), may hold values from 0.3 to 0.9
- pairs: int32 [512, 40], P(('gx', 'gy')), may hold values from 0 to 511, as said below
- home: int32 [512], replicated, may hold values from 0 to 511, as said below
Outputs:
- bounce_one: bfloat16 [512, 75, 128], P(('gx', 'gy'))
- bounce_two: bfloat16 [512, 75, 128], P(('gx', 'gy'))
- energies: float32 [2], replicated
Inputs may be any that keep to these rules, and one draw needn't show every extreme that they name: `home`: A permutation; the block in slot s is held by device s // 16, devices counted gx major. `pairs`: the first 16 entries of a row name blocks held by the same device as the row's slot, the other 24 name blocks held by other devices. Over the rows of one device, the far entries name at most 2 distinct blocks of any one other device, and exactly 2 of some. Ids may repeat within a row; each entry counts.
All inputs are finite; a program needn't handle non-finite values.
Results may differ from a plain program's by a relative error of at most 0.02.
Values may be sent and summed in bfloat16 or wider, within the bound.
A program may use at most 128 MiB of HBM per device.

v0:
```python
import jax
import jax.numpy as jnp
from jax import lax
from jax.sharding import PartitionSpec as P

COLORS = 3
NEAR = 16
CAP = 2
batch_blocks = 4


def form_tiles(recv_pos, recv_nrm, src_pos, src_nrm, src_area):
    distance = None
    along_p = None
    along_q = None
    for axis_id in range(3):
        gap_vec = src_pos[:, :, axis_id, None, :] - recv_pos[:, None, axis_id, :, None]
        near_term = recv_nrm[:, None, axis_id, :, None] * gap_vec
        far_term = src_nrm[:, :, axis_id, None, :] * gap_vec
        if distance is None:
            distance = gap_vec * gap_vec
            along_p = near_term
            along_q = far_term
        else:
            distance = distance + gap_vec * gap_vec
            along_p = along_p + near_term
            along_q = along_q + far_term
    soft_sq = distance + 1.0
    transfer_factors = (
        jnp.maximum(along_p, 0.0)
        * jnp.maximum(-along_q, 0.0)
        * src_area[:, :, None, :]
        / (jnp.pi * soft_sq * soft_sq)
    )
    return transfer_factors.astype(jnp.bfloat16)


def build_tiles(src_positions, src_normals, src_area, pair_row_list, recv_positions, recv_normals):
    turns = pair_row_list.shape[0] // batch_blocks

    def group_tiles(group_id):
        first_row = group_id * batch_blocks
        picked_rows = lax.dynamic_slice_in_dim(pair_row_list, first_row, batch_blocks, 0)
        recv_pos = lax.dynamic_slice_in_dim(recv_positions, first_row, batch_blocks, 0)
        recv_nrm = lax.dynamic_slice_in_dim(recv_normals, first_row, batch_blocks, 0)
        return form_tiles(
            recv_pos,
            recv_nrm,
            jnp.take(src_positions, picked_rows, axis=0),
            jnp.take(src_normals, picked_rows, axis=0),
            jnp.take(src_area, picked_rows, axis=0),
        )

    return lax.map(group_tiles, jnp.arange(turns, dtype=jnp.int32))


def apply_tiles(source_rows, pair_row_list, tiles):
    turns = tiles.shape[0]
    grouped_rows = pair_row_list.reshape((turns, batch_blocks) + pair_row_list.shape[1:])

    def group_term(operands):
        picked_rows, transfer_factors = operands
        collected_values = jnp.take(source_rows, picked_rows, axis=0)
        return jnp.einsum(
            "wxmy,wxsy->wms", collected_values, transfer_factors, preferred_element_type=jnp.float32
        )

    summed = lax.map(group_term, (grouped_rows, tiles))
    return summed.reshape((pair_row_list.shape[0],) + source_rows.shape[1:])


def apply_albedo(summed, albedo):
    blocks_here, channels, verts = summed.shape
    shaped = summed.reshape(blocks_here, COLORS, channels // COLORS, verts) * albedo[:, :, None, :]
    return shaped.reshape(blocks_here, channels, verts)


def total_energy(local_part):
    return lax.psum(local_part, ("gx", "gy"))


def body(transfer, positions, normals, area, albedo, pairs, home):
    devices_all = lax.axis_size(("gx", "gy"))
    device_id = lax.axis_index(("gx", "gy"))
    per_device = transfer.shape[0]
    slot_ids = jnp.take(home, pairs, axis=0)
    near_rows = slot_ids[:, :NEAR] - device_id * per_device
    distant_slot_ids = slot_ids[:, NEAR:]
    owner_dev = distant_slot_ids // per_device
    flat_need = (
        jnp.zeros((devices_all * per_device,), jnp.int32).at[distant_slot_ids.reshape(-1)].max(1)
    )
    needed = flat_need.reshape(devices_all, per_device)
    rank_in_owner = jnp.cumsum(needed, axis=1) - 1
    picked = (
        (needed[:, :, None] == 1)
        & (rank_in_owner[:, :, None] == jnp.arange(CAP, dtype=jnp.int32)[None, None, :])
    ).astype(jnp.int32)
    filled = jnp.sum(picked, axis=1)
    request_list = jnp.sum(
        picked * jnp.arange(per_device, dtype=jnp.int32)[None, :, None], axis=1
    ) + per_device * (1 - filled)
    far_rows = owner_dev * CAP + jnp.take(rank_in_owner.reshape(-1), distant_slot_ids)
    incident_radiance = lax.all_to_all(
        request_list, ("gx", "gy"), split_axis=0, concat_axis=0, tiled=True
    )
    is_filled = incident_radiance < per_device
    chosen = jnp.minimum(incident_radiance, per_device - 1)

    def outbound(table):
        collected_values = jnp.take(table, chosen, axis=0)
        retain_mask = is_filled.reshape(is_filled.shape + (1,) * (table.ndim - 1))
        return jnp.where(retain_mask, collected_values, jnp.zeros((), table.dtype))

    def direct_table(table):
        return table.reshape((devices_all * CAP,) + table.shape[2:])

    near_tiles = build_tiles(positions, normals, area, near_rows, positions, normals)
    near_first = apply_tiles(transfer, near_rows, near_tiles)
    exitant_radiance = (outbound(transfer), outbound(positions), outbound(normals), outbound(area))
    arrived = (
        lax.all_to_all(exitant_radiance[0], ("gx", "gy"), split_axis=0, concat_axis=0, tiled=True),
        lax.all_to_all(
            exitant_radiance[1].astype(jnp.bfloat16),
            ("gx", "gy"),
            split_axis=0,
            concat_axis=0,
            tiled=True,
        ).astype(jnp.float32),
        lax.all_to_all(
            exitant_radiance[2].astype(jnp.bfloat16),
            ("gx", "gy"),
            split_axis=0,
            concat_axis=0,
            tiled=True,
        ).astype(jnp.float32),
        lax.all_to_all(
            exitant_radiance[3].astype(jnp.bfloat16),
            ("gx", "gy"),
            split_axis=0,
            concat_axis=0,
            tiled=True,
        ).astype(jnp.float32),
    )
    table_transfer = direct_table(arrived[0])
    table_pos = direct_table(arrived[1])
    table_nrm = direct_table(arrived[2])
    table_area = direct_table(arrived[3])
    far_tiles = build_tiles(table_pos, table_nrm, table_area, far_rows, positions, normals)
    far_first = apply_tiles(table_transfer, far_rows, far_tiles)
    first_bounce = apply_albedo(near_first + far_first, albedo)
    bounce_one = first_bounce.astype(jnp.bfloat16)
    local_one = jnp.sum(area[:, None, :] * first_bounce * first_bounce)
    near_second = apply_tiles(bounce_one, near_rows, near_tiles)
    second_table = direct_table(
        lax.all_to_all(outbound(bounce_one), ("gx", "gy"), split_axis=0, concat_axis=0, tiled=True)
    )
    far_second = apply_tiles(second_table, far_rows, far_tiles)
    second_bounce = apply_albedo(near_second + far_second, albedo)
    bounce_two = second_bounce.astype(jnp.bfloat16)
    local_two = jnp.sum(area[:, None, :] * second_bounce * second_bounce)
    energy_one = total_energy(local_one)
    energy_two = total_energy(local_two)
    inv_count = 1.0 / (devices_all * per_device * transfer.shape[2] * transfer.shape[1])
    energies = jnp.stack([energy_one, energy_two]) * inv_count
    return (bounce_one, bounce_two, energies)


def solution(mesh):
    return jax.shard_map(
        body,
        mesh=mesh,
        in_specs=(
            P(("gx", "gy"), None, None),
            P(("gx", "gy"), None, None),
            P(("gx", "gy"), None, None),
            P(("gx", "gy"), None),
            P(("gx", "gy"), None, None),
            P(("gx", "gy"), None),
            P(),
        ),
        out_specs=(P(("gx", "gy"), None, None), P(("gx", "gy"), None, None), P()),
        check_vma=False,
    )
```

profile of v0, /device:TPU:0, one launch (start us, length us, event | category | flops | bytes accessed | tf_op | source)
XLA Modules:
  0.0 292.2 jit_solution(17152638488114444716)
XLA Ops:
  1.5 4.3 %gather_fusion.10 = s32[640]{0:T(1024)S(1)} fusion(s32[512]{0:T(512)S(1)} %copy-done, s32[1024]{0:T(1024)S(1)} %pad_clamp_fusion.9), kind=kCustom, calls=%fused_computation.14 | custom fusion | bytes 7680 | tf_op jit(solution)/shard_map/jit(_take)/gather | solution.py:86
  6.1 3.9 %scatter_custom_fusion = s32[512]{0:T(512)S(1)} fusion(s32[384]{0:T(512)S(1)} %fusion.94, s32[384]{0:T(512)S(1)} %broadcast.438, s32[]{:T(128)} %copy.344), kind=kCustom, calls=%fused_computation.200 | custom fusion | flops 384 | bytes 2052 | tf_op jit(solution)/shard_map/scatter-max | solution.py:91
  11.2 7.3 %all-to-all-start = ((s32[32,1,2]{2,1,0:T(1,128)}), s32[32,1,2]{2,1,0:T(1,128)S(1)}, u32[]{:S(2)}, u32[]{:S(2)}) async-start(s32[32,1,2]{2,1,0:T(1,128)} %copy.220), calls=%async_computation | async-start | bytes 32768 | tf_op jit(solution)/shard_map/all_to_all | solution.py:104
  18.7 2.8 gather_fusion.11
  21.7 38.1 %while.60 = (s32[]{:T(128)}, bf16[4,4,16,128,128]{4,3,2,1,0:T(8,128)(2,1)}, s32[4]{0:T(128)S(1)}, f32[16,3,128]{2,1,0:T(4,128)S(1)}, s32[16,16]{1,0:T(8,128)S(1)...) while((s32[]{:T(128)}, ...), condition=%wide.region_1.3_spmd, body=%wide.region_0.0_spmd.sunk | while | flops 29418888 | bytes 3681183 | solution.py:54
  25.4 5.8 %fusion.115 = bf16[4,4,16,128,128]{4,3,2,1,0:T(8,128)(2,1)} fusion(bf16[4,4,16,128,128]{4,3,2,1,0:T(8,128)(2,1)} %get-tuple-element.810, s32[]{:T(128)} %get-tuple-element.809, f32[4,16,128]{2,1,0:T(8,128)S(1)} %broadcast_select_fusion.11, f32[4,16,128]{2,1,0:T(8,128)S(1)} %bitcast.220, f32[4,16,128]{2,1,0:T(8,128)S(1)} %bitcast.219, ...), kind=kLoop, calls=%fused_computation.42.clone.1 | loop fusion | flops 29360128 | bytes 2339328 | tf_op jit(solution)/shard_map/while/body/jit(dynamic_update_index_in_dim)/dynamic_update_slice | solution.py:54
  35.0 5.8 %fusion.115 = bf16[4,4,16,128,128]{4,3,2,1,0:T(8,128)(2,1)} fusion(bf16[4,4,16,128,128]{4,3,2,1,0:T(8,128)(2,1)} %get-tuple-element.810, s32[]{:T(128)} %get-tuple-element.809, f32[4,16,128]{2,1,0:T(8,128)S(1)} %broadcast_select_fusion.11, f32[4,16,128]{2,1,0:T(8,128)S(1)} %bitcast.220, f32[4,16,128]{2,1,0:T(8,128)S(1)} %bitcast.219, ...), kind=kLoop, calls=%fused_computation.42.clone.1 | loop fusion | flops 29360128 | bytes 2339328 | tf_op jit(solution)/shard_map/while/body/jit(dynamic_update_index_in_dim)/dynamic_update_slice | solution.py:54
  44.5 5.8 %fusion.115 = bf16[4,4,16,128,128]{4,3,2,1,0:T(8,128)(2,1)} fusion(bf16[4,4,16,128,128]{4,3,2,1,0:T(8,128)(2,1)} %get-tuple-element.810, s32[]{:T(128)} %get-tuple-element.809, f32[4,16,128]{2,1,0:T(8,128)S(1)} %broadcast_select_fusion.11, f32[4,16,128]{2,1,0:T(8,128)S(1)} %bitcast.220, f32[4,16,128]{2,1,0:T(8,128)S(1)} %bitcast.219, ...), kind=kLoop, calls=%fused_computation.42.clone.1 | loop fusion | flops 29360128 | bytes 2339328 | tf_op jit(solution)/shard_map/while/body/jit(dynamic_update_index_in_dim)/dynamic_update_slice | solution.py:54
  54.0 5.8 %fusion.115 = bf16[4,4,16,128,128]{4,3,2,1,0:T(8,128)(2,1)} fusion(bf16[4,4,16,128,128]{4,3,2,1,0:T(8,128)(2,1)} %get-tuple-element.810, s32[]{:T(128)} %get-tuple-element.809, f32[4,16,128]{2,1,0:T(8,128)S(1)} %broadcast_select_fusion.11, f32[4,16,128]{2,1,0:T(8,128)S(1)} %bitcast.220, f32[4,16,128]{2,1,0:T(8,128)S(1)} %bitcast.219, ...), kind=kLoop, calls=%fused_computation.42.clone.1 | loop fusion | flops 29360128 | bytes 2339328 | tf_op jit(solution)/shard_map/while/body/jit(dynamic_update_index_in_dim)/dynamic_update_slice | solution.py:54
  60.0 14.0 %while.61 = (s32[]{:T(128)}, f32[4,4,75,128]{3,1,0,2:T(4,128)S(1)}, s32[4,4,16]{2,1,0:T(4,128)S(1)}, bf16[16,75,128]{2,1,0:T(8,128)(2,1)S(1)}, bf16[4,4,16,128,128]{4,3,2,1,0:T(8,128)(2,1)}, /*index=5*/s32[]{:T(128)}) while((s32[]{:T(128)}, f32[4,4,75,128]{3,1,0,2:T(4,128)S(1)}, s32[4,4,16]{2,1,0:T(4,128)S(1)}, ...), condition=%wide.region_3.6_spmd, body=%wide.region_2.5_spmd.sunk | while | flops 157902208 | bytes 6260941 | solution.py:68
  60.9 2.5 fusion.118
  64.4 2.5 fusion.118
  67.9 2.5 fusion.118
  71.4 2.5 fusion.118
  77.6 6.0 %all-to-all-start.4 = ((bf16[32,2,128]{2,1,0:T(2,128)(2,1)}), bf16[32,2,128]{2,1,0:T(2,128)(2,1)S(1)}, u32[]{:S(2)}, u32[]{:S(2)}) async-start(bf16[32,2,128]{2,1,0:T(2,128)(2,1)} %select_convert_fusion), calls=%async_computation.4 | async-start | bytes 32768 | tf_op jit(solution)/shard_map/all_to_all | solution.py:137
  84.5 5.4 %gather_fusion.13 = bf16[64,75,128]{2,0,1:T(8,128)(2,1)S(1)} fusion(bf16[16,75,128]{2,0,1:T(8,128)(2,1)S(1)} %copy-done.1, s32[1024]{0:T(1024)S(1)} %pad_clamp_fusion.7), kind=kCustom, calls=%fused_computation.4.clone | custom fusion | bytes 2457856 | tf_op jit(solution)/shard_map/jit(_take)/gather | solution.py:111
  90.6 5.0 %all-to-all-start.2 = ((bf16[32,2,3,128]{3,1,2,0:T(2,128)(2,1)}), bf16[32,2,3,128]{3,1,2,0:T(2,128)(2,1)S(1)}, u32[]{:S(2)}, u32[]{:S(2)}) async-start(bf16[32,2,3,128]{3,1,2,0:T(2,128)(2,1)} %get-tuple-element.491), calls=%async_computation.2 | async-start | bytes 98304 | tf_op jit(solution)/shard_map/all_to_all | solution.py:123
  95.6 2.5 broadcast_select_fusion.7
  98.1 4.7 %all-to-all-done.2 = bf16[32,2,3,128]{3,1,2,0:T(2,128)(2,1)S(1)} async-done(((bf16[32,2,3,128]{3,1,2,0:T(2,128)(2,1)}), bf16[32,2,3,128]{3,1,2,0:T(2,128)(2,1)S(1)}, u32[]{:S(2)}, u32[]{:S(2)}) %all-to-all-start.2) | async-done | bytes 49184 | tf_op jit(solution)/shard_map/all_to_all | solution.py:123
  102.9 2.6 all-to-all-start.3
  105.6 7.1 %all-to-all-done.3 = bf16[32,2,3,128]{3,1,2,0:T(2,128)(2,1)S(1)} async-done(((bf16[32,2,3,128]{3,1,2,0:T(2,128)(2,1)}), bf16[32,2,3,128]{3,1,2,0:T(2,128)(2,1)S(1)}, u32[]{:S(2)}, u32[]{:S(2)}) %all-to-all-start.3) | async-done | bytes 49184 | tf_op jit(solution)/shard_map/all_to_all | solution.py:130
  112.7 2.9 all-to-all-start.1
  115.8 43.3 %while.62 = (s32[]{:T(128)}, bf16[4,4,24,128,128]{4,3,2,1,0:T(8,128)(2,1)}, s32[4]{0:T(128)S(1)}, f32[16,3,128]{2,0,1:T(8,128)S(1)}, s32[16,24]{1,0:T(8,128)S(1)...) while((s32[]{:T(128)}, ...), condition=%wide.region_9.14_spmd, body=%wide.region_8.13_spmd.sunk | while | flops 44127816 | bytes 5500943 | solution.py:54
  119.4 7.2 %fusion.119 = bf16[4,4,24,128,128]{4,3,2,1,0:T(8,128)(2,1)} fusion(bf16[4,4,24,128,128]{4,3,2,1,0:T(8,128)(2,1)} %get-tuple-element.869, s32[]{:T(128)} %get-tuple-element.868, f32[4,24,128]{2,1,0:T(8,128)S(1)} %broadcast_select_fusion.13, f32[4,24,128]{2,1,0:T(8,128)S(1)} %get-tuple-element.763, f32[4,24,128]{2,1,0:T(8,128)S(1)} %get-tuple-element.764, ...), kind=kLoop, calls=%fused_computation.92.clone.1 | loop fusion | flops 44040192 | bytes 3502592 | tf_op jit(solution)/shard_map/while/body/jit(dynamic_update_index_in_dim)/dynamic_update_slice | solution.py:54
  130.2 7.2 %fusion.119 = bf16[4,4,24,128,128]{4,3,2,1,0:T(8,128)(2,1)} fusion(bf16[4,4,24,128,128]{4,3,2,1,0:T(8,128)(2,1)} %get-tuple-element.869, s32[]{:T(128)} %get-tuple-element.868, f32[4,24,128]{2,1,0:T(8,128)S(1)} %broadcast_select_fusion.13, f32[4,24,128]{2,1,0:T(8,128)S(1)} %get-tuple-element.763, f32[4,24,128]{2,1,0:T(8,128)S(1)} %get-tuple-element.764, ...), kind=kLoop, calls=%fused_computation.92.clone.1 | loop fusion | flops 44040192 | bytes 3502592 | tf_op jit(solution)/shard_map/while/body/jit(dynamic_update_index_in_dim)/dynamic_update_slice | solution.py:54
  141.0 7.2 %fusion.119 = bf16[4,4,24,128,128]{4,3,2,1,0:T(8,128)(2,1)} fusion(bf16[4,4,24,128,128]{4,3,2,1,0:T(8,128)(2,1)} %get-tuple-element.869, s32[]{:T(128)} %get-tuple-element.868, f32[4,24,128]{2,1,0:T(8,128)S(1)} %broadcast_select_fusion.13, f32[4,24,128]{2,1,0:T(8,128)S(1)} %get-tuple-element.763, f32[4,24,128]{2,1,0:T(8,128)S(1)} %get-tuple-element.764, ...), kind=kLoop, calls=%fused_computation.92.clone.1 | loop fusion | flops 44040192 | bytes 3502592 | tf_op jit(solution)/shard_map/while/body/jit(dynamic_update_index_in_dim)/dynamic_update_slice | solution.py:54
  151.9 7.2 %fusion.119 = bf16[4,4,24,128,128]{4,3,2,1,0:T(8,128)(2,1)} fusion(bf16[4,4,24,128,128]{4,3,2,1,0:T(8,128)(2,1)} %get-tuple-element.869, s32[]{:T(128)} %get-tuple-element.868, f32[4,24,128]{2,1,0:T(8,128)S(1)} %broadcast_select_fusion.13, f32[4,24,128]{2,1,0:T(8,128)S(1)} %get-tuple-element.763, f32[4,24,128]{2,1,0:T(8,128)S(1)} %get-tuple-element.764, ...), kind=kLoop, calls=%fused_computation.92.clone.1 | loop fusion | flops 44040192 | bytes 3502592 | tf_op jit(solution)/shard_map/while/body/jit(dynamic_update_index_in_dim)/dynamic_update_slice | solution.py:54
  162.2 19.7 %while.63 = (s32[]{:T(128)}, f32[4,4,75,128]{3,1,0,2:T(4,128)}, s32[4,4,24]{2,1,0:T(4,128)S(1)}, bf16[64,75,128]{2,1,0:T(8,128)(2,1)S(1)}, bf16[4,4,24,128,128]{4,3,2,1,0:T(8,128)(2,1)}, /*index=5*/s32[]{:T(128)}) while((s32[]{:T(128)}, f32[4,4,75,128]{3,1,0,2:T(4,128)}, s32[4,4,24]{2,1,0:T(4,128)S(1)}, ...), condition=%wide.region_11.18_spmd, body=%wide.region_10.17_spmd.sunk | while | flops 236852800 | bytes 9143817 | solution.py:68
  163.2 3.1 %fusion.122 = f32[1,4,75,128]{3,2,1,0:T(8,128)S(1)} fusion(bf16[4,4,24,128,128]{4,3,2,1,0:T(8,128)(2,1)} %get-tuple-element.914, s32[]{:T(128)} %get-tuple-element.904, bf16[4,24,75,128]{3,2,1,0:T(8,128)(2,1)S(1)} %bitcast.201, pred[4,24]{1,0:T(4,128)(4,1)S(1)} %get-tuple-element.781), kind=kOutput, calls=%fused_computation.116.clone.1 | convolution fusion | flops 236851200 | bytes 5143136 | tf_op jit(solution)/shard_map/while/body/eval_jaxpr/wxmy,wxsy->wms/dot_general | solution.py:64
  168.1 3.1 %fusion.122 = f32[1,4,75,128]{3,2,1,0:T(8,128)S(1)} fusion(bf16[4,4,24,128,128]{4,3,2,1,0:T(8,128)(2,1)} %get-tuple-element.914, s32[]{:T(128)} %get-tuple-element.904, bf16[4,24,75,128]{3,2,1,0:T(8,128)(2,1)S(1)} %bitcast.201, pred[4,24]{1,0:T(4,128)(4,1)S(1)} %get-tuple-element.781), kind=kOutput, calls=%fused_computation.116.clone.1 | convolution fusion | flops 236851200 | bytes 5143136 | tf_op jit(solution)/shard_map/while/body/eval_jaxpr/wxmy,wxsy->wms/dot_general | solution.py:64
  173.0 3.1 %fusion.122 = f32[1,4,75,128]{3,2,1,0:T(8,128)S(1)} fusion(bf16[4,4,24,128,128]{4,3,2,1,0:T(8,128)(2,1)} %get-tuple-element.914, s32[]{:T(128)} %get-tuple-element.904, bf16[4,24,75,128]{3,2,1,0:T(8,128)(2,1)S(1)} %bitcast.201, pred[4,24]{1,0:T(4,128)(4,1)S(1)} %get-tuple-element.781), kind=kOutput, calls=%fused_computation.116.clone.1 | convolution fusion | flops 236851200 | bytes 5143136 | tf_op jit(solution)/shard_map/while/body/eval_jaxpr/wxmy,wxsy->wms/dot_general | solution.py:64
  177.9 3.1 %fusion.122 = f32[1,4,75,128]{3,2,1,0:T(8,128)S(1)} fusion(bf16[4,4,24,128,128]{4,3,2,1,0:T(8,128)(2,1)} %get-tuple-element.914, s32[]{:T(128)} %get-tuple-element.904, bf16[4,24,75,128]{3,2,1,0:T(8,128)(2,1)S(1)} %bitcast.201, pred[4,24]{1,0:T(4,128)(4,1)S(1)} %get-tuple-element.781), kind=kOutput, calls=%fused_computation.116.clone.1 | convolution fusion | flops 236851200 | bytes 5143136 | tf_op jit(solution)/shard_map/while/body/eval_jaxpr/wxmy,wxsy->wms/dot_general | solution.py:64
  186.7 2.6 broadcast_select_fusion.6
  189.3 5.9 %all-to-all-start.5 = ((bf16[32,2,75,128]{3,1,2,0:T(2,128)(2,1)}), bf16[32,2,75,128]{3,1,2,0:T(2,128)(2,1)S(1)}, u32[]{:S(2)}, u32[]{:S(2)}) async-start(bf16[32,2,75,128]{3,1,2,0:T(2,128)(2,1)} %broadcast_select_fusion.6), calls=%async_computation.5 | async-start | bytes 2457600 | tf_op jit(solution)/shard_map/all_to_all | solution.py:156
  195.3 14.0 %while.64 = (s32[]{:T(128)}, f32[4,4,75,128]{3,1,0,2:T(4,128)S(1)}, s32[4,4,16]{2,1,0:T(4,128)S(1)}, bf16[16,75,128]{2,1,0:T(8,128)(2,1)S(1)}, bf16[4,4,16,128,128]{4,3,2,1,0:T(8,128)(2,1)}, /*index=5*/s32[]{:T(128)}) while((s32[]{:T(128)}, f32[4,4,75,128]{3,1,0,2:T(4,128)S(1)}, s32[4,4,16]{2,1,0:T(4,128)S(1)}, ...), condition=%wide.region_13.20_spmd, body=%wide.region_12.19_spmd.sunk | while | flops 157902208 | bytes 6260941 | solution.py:68
  196.2 2.5 fusion.125
  199.7 2.5 fusion.125
  203.2 2.5 fusion.125
  206.7 2.5 fusion.125
  209.3 16.9 %all-to-all-done.5 = bf16[32,2,75,128]{3,1,2,0:T(2,128)(2,1)S(1)} async-done(((bf16[32,2,75,128]{3,1,2,0:T(2,128)(2,1)}), bf16[32,2,75,128]{3,1,2,0:T(2,128)(2,1)S(1)}, u32[]{:S(2)}, u32[]{:S(2)}) %all-to-all-start.5) | async-done | bytes 1228832 | tf_op jit(solution)/shard_map/all_to_all | solution.py:156
  229.3 19.6 %while.65 = (s32[]{:T(128)}, f32[4,4,75,128]{3,1,0,2:T(4,128)}, s32[4,4,24]{2,1,0:T(4,128)S(1)}, bf16[64,75,128]{2,1,0:T(8,128)(2,1)S(1)}, bf16[4,4,24,128,128]{4,3,2,1,0:T(8,128)(2,1)}, /*index=5*/s32[]{:T(128)}) while((s32[]{:T(128)}, f32[4,4,75,128]{3,1,0,2:T(4,128)}, s32[4,4,24]{2,1,0:T(4,128)S(1)}, ...), condition=%wide.region_15.22_spmd, body=%wide.region_14.21_spmd.sunk | while | flops 236852800 | bytes 9143817 | solution.py:68
  230.4 3.1 %fusion.128 = f32[1,4,75,128]{3,2,1,0:T(8,128)S(1)} fusion(bf16[4,4,24,128,128]{4,3,2,1,0:T(8,128)(2,1)} %get-tuple-element.950, s32[]{:T(128)} %get-tuple-element.940, bf16[4,24,75,128]{3,2,1,0:T(8,128)(2,1)S(1)} %bitcast.202, pred[4,24]{1,0:T(4,128)(4,1)S(1)} %get-tuple-element.795), kind=kOutput, calls=%fused_computation.142.clone.1 | convolution fusion | flops 236851200 | bytes 5143136 | tf_op jit(solution)/shard_map/while/body/eval_jaxpr/wxmy,wxsy->wms/dot_general | solution.py:64
  235.3 3.1 %fusion.128 = f32[1,4,75,128]{3,2,1,0:T(8,128)S(1)} fusion(bf16[4,4,24,128,128]{4,3,2,1,0:T(8,128)(2,1)} %get-tuple-element.950, s32[]{:T(128)} %get-tuple-element.940, bf16[4,24,75,128]{3,2,1,0:T(8,128)(2,1)S(1)} %bitcast.202, pred[4,24]{1,0:T(4,128)(4,1)S(1)} %get-tuple-element.795), kind=kOutput, calls=%fused_computation.142.clone.1 | convolution fusion | flops 236851200 | bytes 5143136 | tf_op jit(solution)/shard_map/while/body/eval_jaxpr/wxmy,wxsy->wms/dot_general | solution.py:64
  240.2 3.1 %fusion.128 = f32[1,4,75,128]{3,2,1,0:T(8,128)S(1)} fusion(bf16[4,4,24,128,128]{4,3,2,1,0:T(8,128)(2,1)} %get-tuple-element.950, s32[]{:T(128)} %get-tuple-element.940, bf16[4,24,75,128]{3,2,1,0:T(8,128)(2,1)S(1)} %bitcast.202, pred[4,24]{1,0:T(4,128)(4,1)S(1)} %get-tuple-element.795), kind=kOutput, calls=%fused_computation.142.clone.1 | convolution fusion | flops 236851200 | bytes 5143136 | tf_op jit(solution)/shard_map/while/body/eval_jaxpr/wxmy,wxsy->wms/dot_general | solution.py:64
  245.1 3.1 %fusion.128 = f32[1,4,75,128]{3,2,1,0:T(8,128)S(1)} fusion(bf16[4,4,24,128,128]{4,3,2,1,0:T(8,128)(2,1)} %get-tuple-element.950, s32[]{:T(128)} %get-tuple-element.940, bf16[4,24,75,128]{3,2,1,0:T(8,128)(2,1)S(1)} %bitcast.202, pred[4,24]{1,0:T(4,128)(4,1)S(1)} %get-tuple-element.795), kind=kOutput, calls=%fused_computation.142.clone.1 | convolution fusion | flops 236851200 | bytes 5143136 | tf_op jit(solution)/shard_map/while/body/eval_jaxpr/wxmy,wxsy->wms/dot_general | solution.py:64
  248.9 2.7 fusion.83
  252.4 37.9 %all-reduce = (f32[1]{0:T(128)}, f32[1]{0:T(128)}) all-reduce(f32[1]{0:T(128)} %bitcast.78, f32[1]{0:T(128)} %bitcast.77), channel_id=1, replica_groups=mesh['gx'=4,'gy'=8] {'gx','gy'}, use_global_device_ids=true, to_apply=%region_19.26 | all-reduce | flops 2 | bytes 16 | tf_op jit(solution)/shard_map/psum | solution.py:79
  290.4 1.8 maximum_multiply_fusion
  (264 shorter events, 65.9 us)
Async XLA Ops:
  0.6 0.8 copy-start
  1.5 4.4 %copy-start.10 = (s32[16,40]{1,0:T(8,128)S(1)}, s32[16,40]{1,0:T(8,128)}, u32[]{:S(2)}) copy-start(s32[16,40]{1,0:T(8,128)} %param.36) | copy-start | bytes 7684
  11.2 63.0 %all-to-all-start = ((s32[32,1,2]{2,1,0:T(1,128)}), s32[32,1,2]{2,1,0:T(1,128)S(1)}, u32[]{:S(2)}, u32[]{:S(2)}) async-start(s32[32,1,2]{2,1,0:T(1,128)} %copy.220), calls=%async_computation | async-start | bytes 32768 | tf_op jit(solution)/shard_map/all_to_all | solution.py:104
  18.7 3.0 %copy-start.3 = (f32[16,3,128]{2,0,1:T(8,128)S(1)}, f32[16,3,128]{2,0,1:T(8,128)}, u32[]{:S(2)}) copy-start(f32[16,3,128]{2,0,1:T(8,128)} %param.33) | copy-start | bytes 73732
  18.7 3.0 %copy-start.4 = (f32[16,3,128]{2,0,1:T(8,128)S(1)}, f32[16,3,128]{2,0,1:T(8,128)}, u32[]{:S(2)}) copy-start(f32[16,3,128]{2,0,1:T(8,128)} %param.32) | copy-start | bytes 73732
  18.7 3.0 %copy-start.2 = (f32[16,128]{1,0:T(8,128)S(1)}, f32[16,128]{1,0:T(8,128)}, u32[]{:S(2)}) copy-start(f32[16,128]{1,0:T(8,128)} %param.34) | copy-start | bytes 24580
  21.7 38.1 %copy-start.1 = (bf16[16,75,128]{2,0,1:T(8,128)(2,1)S(1)}, bf16[16,75,128]{2,0,1:T(8,128)(2,1)}, u32[]{:S(2)}) copy-start(bf16[16,75,128]{2,0,1:T(8,128)(2,1)} %param.31) | copy-start | bytes 921604
  74.0 15.9 %copy-start.7 = (f32[4,4,75,128]{3,1,0,2:T(4,128)}, f32[4,4,75,128]{3,1,0,2:T(4,128)S(1)}, u32[]{:S(2)}) copy-start(f32[4,4,75,128]{3,1,0,2:T(4,128)S(1)} %get-tuple-element.202) | copy-start | bytes 1843204
  77.6 13.0 %all-to-all-start.4 = ((bf16[32,2,128]{2,1,0:T(2,128)(2,1)}), bf16[32,2,128]{2,1,0:T(2,128)(2,1)S(1)}, u32[]{:S(2)}, u32[]{:S(2)}) async-start(bf16[32,2,128]{2,1,0:T(2,128)(2,1)} %select_convert_fusion), calls=%async_computation.4 | async-start | bytes 32768 | tf_op jit(solution)/shard_map/all_to_all | solution.py:137
  90.6 12.2 %all-to-all-start.2 = ((bf16[32,2,3,128]{3,1,2,0:T(2,128)(2,1)}), bf16[32,2,3,128]{3,1,2,0:T(2,128)(2,1)S(1)}, u32[]{:S(2)}, u32[]{:S(2)}) async-start(bf16[32,2,3,128]{3,1,2,0:T(2,128)(2,1)} %get-tuple-element.491), calls=%async_computation.2 | async-start | bytes 98304 | tf_op jit(solution)/shard_map/all_to_all | solution.py:123
  102.9 9.8 %all-to-all-start.3 = ((bf16[32,2,3,128]{3,1,2,0:T(2,128)(2,1)}), bf16[32,2,3,128]{3,1,2,0:T(2,128)(2,1)S(1)}, u32[]{:S(2)}, u32[]{:S(2)}) async-start(bf16[32,2,3,128]{3,1,2,0:T(2,128)(2,1)} %get-tuple-element.490), calls=%async_computation.3 | async-start | bytes 98304 | tf_op jit(solution)/shard_map/all_to_all | solution.py:130
  112.7 46.4 %all-to-all-start.1 = ((bf16[32,2,75,128]{3,1,2,0:T(2,128)(2,1)}), bf16[32,2,75,128]{3,1,2,0:T(2,128)(2,1)S(1)}, u32[]{:S(2)}, u32[]{:S(2)}) async-start(bf16[32,2,75,128]{3,1,2,0:T(2,128)(2,1)} %broadcast_select_fusion.7), calls=%async_computation.1 | async-start | bytes 2457600 | tf_op jit(solution)/shard_map/all_to_all | solution.py:122
  162.2 21.3 %copy-start.9 = (f32[16,3,128]{2,0,1:T(8,128)S(1)}, f32[16,3,128]{2,0,1:T(8,128)}, u32[]{:S(2)}) copy-start(f32[16,3,128]{2,0,1:T(8,128)} %param.35) | copy-start | bytes 73732
  183.2 0.8 copy-start.5
  184.1 0.8 copy-start.6
  189.3 37.0 %all-to-all-start.5 = ((bf16[32,2,75,128]{3,1,2,0:T(2,128)(2,1)}), bf16[32,2,75,128]{3,1,2,0:T(2,128)(2,1)S(1)}, u32[]{:S(2)}, u32[]{:S(2)}) async-start(bf16[32,2,75,128]{3,1,2,0:T(2,128)(2,1)} %broadcast_select_fusion.6), calls=%async_computation.5 | async-start | bytes 2457600 | tf_op jit(solution)/shard_map/all_to_all | solution.py:156
  209.3 20.0 %copy-start.8 = (f32[4,4,75,128]{3,1,0,2:T(4,128)}, f32[4,4,75,128]{3,1,0,2:T(4,128)S(1)}, u32[]{:S(2)}) copy-start(f32[4,4,75,128]{3,1,0,2:T(4,128)S(1)} %get-tuple-element.205) | copy-start | bytes 1843204
where the time goes:
time: 293 us; the launch traced here: 292 us
  other arithmetic  72.8 us (25%)
  local copies, waits for them, and re-layouts  70.6 us (24%)
  matrix products  44.8 us (15%)
  blocking collectives  37.9 us (13%)
  starting transfers between devices  29.7 us (10%)
  waiting for transfers between devices  29.4 us (10%)
  loops' own time  5.88 us (2%)
    dynamic_update_slice x8, other arithmetic, build_tiles(): return lax.map(group_tiles, jnp.arange(turns, dtype=jnp.int32))  52.1 us
    dot_general x16, matrix products, group_term(): jnp.einsum('wxmy,wxsy->wms', collected_values, transfer_factors, preferre...  44.8 us
    psum x1, blocking collectives, total_energy(): return lax.psum(local_part, ('gx', 'gy'))  37.9 us
    all_to_all x1, waiting for transfers between devices, body(): lax.all_to_all(outbound(bounce_one), ('gx', 'gy'), split_axis=0, concat_a...  16.9 us
    gather x16, local copies, waits for them, and re-layouts, group_term(): collected_values = jnp.take(source_rows, picked_rows, axis=0)  13.9 us
    gather x5, local copies, waits for them, and re-layouts, outbound(): collected_values = jnp.take(table, chosen, axis=0)  8.2 us
    all_to_all x1, starting transfers between devices, body(): lax.all_to_all(request_list, ('gx', 'gy'), split_axis=0, concat_axis=0, t...  7.33 us
    all_to_all x1, waiting for transfers between devices, body(): lax.all_to_all(exitant_radiance[2].astype(jnp.bfloat16), ('gx', 'gy'), sp...  7.05 us
  transfers between devices with their start and end apart: 6, of which 4 were waited for; matrix products, arithmetic and copies ran while one was open for 40% of the time, Pallas kernels for 0%

commit v1 on v0

--- a/solution.py
+++ b/solution.py
@@ -76,7 +76,7 @@
 
 
 def total_energy(local_part):
-    return lax.psum(local_part, ("gx", "gy"))
+    return lax.psum(lax.psum(local_part, "gy"), "gx")
 
 
 def body(transfer, positions, normals, area, albedo, pairs, home):

time: 293 us -> 281 us (0.959)
  blocking collectives: 37.9 us -> 25.6 us
    psum x1 -> x2, blocking collectives: 37.9 us -> 25.6 us  [total_energy(): return lax.psum(lax.psum(local_part, 'gy'), 'gx')]
  transfers between devices with their start and end apart: 6 -> 6, of which waited for: 4 -> 4; matrix products, arithmetic and copies ran while one was open for 40% -> 42% of each run, Pallas kernels for 0% -> 0%
where the time goes in v1:
time: 281 us; the launch traced here: 280 us
  other arithmetic  75.4 us (27%)
  local copies, waits for them, and re-layouts  70.6 us (25%)
  matrix products  44.7 us (16%)
  starting transfers between devices  29.7 us (11%)
  waiting for transfers between devices  26.8 us (10%)
  blocking collectives  25.6 us (9%)
  loops' own time  5.87 us (2%)
    dynamic_update_slice x8, other arithmetic, build_tiles(): return lax.map(group_tiles, jnp.arange(turns, dtype=jnp.int32))  52.1 us
    dot_general x16, matrix products, group_term(): jnp.einsum('wxmy,wxsy->wms', collected_values, transfer_factors, preferre...  44.7 us
    psum x2, blocking collectives, total_energy(): return lax.psum(lax.psum(local_part, 'gy'), 'gx')  25.6 us
    all_to_all x1, waiting for transfers between devices, body(): lax.all_to_all(outbound(bounce_one), ('gx', 'gy'), split_axis=0, concat_a...  14.3 us
    gather x16, local copies, waits for them, and re-layouts, group_term(): collected_values = jnp.take(source_rows, picked_rows, axis=0)  13.9 us
    gather x5, local copies, waits for them, and re-layouts, outbound(): collected_values = jnp.take(table, chosen, axis=0)  8.2 us
    all_to_all x1, starting transfers between devices, body(): lax.all_to_all(request_list, ('gx', 'gy'), split_axis=0, concat_axis=0, t...  7.33 us
    all_to_all x1, waiting for transfers between devices, body(): lax.all_to_all(exitant_radiance[2].astype(jnp.bfloat16), ('gx', 'gy'), sp...  7.05 us
  transfers between devices with their start and end apart: 6, of which 4 were waited for; matrix products, arithmetic and copies ran while one was open for 42% of the time, Pallas kernels for 0%

profile of v1, /device:TPU:0, one launch (start us, length us, event | category | flops | bytes accessed | tf_op | source)
XLA Modules:
  0.0 279.9 jit_solution(13410324950287861938)
XLA Ops:
  1.5 4.3 %gather_fusion.10 = s32[640]{0:T(1024)S(1)} fusion(s32[512]{0:T(512)S(1)} %copy-done, s32[1024]{0:T(1024)S(1)} %pad_clamp_fusion.9), kind=kCustom, calls=%fused_computation.14 | custom fusion | bytes 7680 | tf_op jit(solution)/shard_map/jit(_take)/gather | solution.py:86
  6.1 3.9 %scatter_custom_fusion = s32[512]{0:T(512)S(1)} fusion(s32[384]{0:T(512)S(1)} %fusion.94, s32[384]{0:T(512)S(1)} %broadcast.438, s32[]{:T(128)} %copy.344), kind=kCustom, calls=%fused_computation.200 | custom fusion | flops 384 | bytes 2052 | tf_op jit(solution)/shard_map/scatter-max | solution.py:91
  11.2 7.3 %all-to-all-start = ((s32[32,1,2]{2,1,0:T(1,128)}), s32[32,1,2]{2,1,0:T(1,128)S(1)}, u32[]{:S(2)}, u32[]{:S(2)}) async-start(s32[32,1,2]{2,1,0:T(1,128)} %copy.220), calls=%async_computation | async-start | bytes 32768 | tf_op jit(solution)/shard_map/all_to_all | solution.py:104
  18.7 2.8 gather_fusion.11
  21.8 38.0 %while.60 = (s32[]{:T(128)}, bf16[4,4,16,128,128]{4,3,2,1,0:T(8,128)(2,1)}, s32[4]{0:T(128)S(1)}, f32[16,3,128]{2,1,0:T(4,128)S(1)}, s32[16,16]{1,0:T(8,128)S(1)...) while((s32[]{:T(128)}, ...), condition=%wide.region_1.3_spmd, body=%wide.region_0.0_spmd.sunk | while | flops 29418888 | bytes 3681183 | solution.py:54
  25.4 5.9 %fusion.115 = bf16[4,4,16,128,128]{4,3,2,1,0:T(8,128)(2,1)} fusion(bf16[4,4,16,128,128]{4,3,2,1,0:T(8,128)(2,1)} %get-tuple-element.812, s32[]{:T(128)} %get-tuple-element.811, f32[4,16,128]{2,1,0:T(8,128)S(1)} %broadcast_select_fusion.11, f32[4,16,128]{2,1,0:T(8,128)S(1)} %bitcast.220, f32[4,16,128]{2,1,0:T(8,128)S(1)} %bitcast.219, ...), kind=kLoop, calls=%fused_computation.42.clone.1 | loop fusion | flops 29360128 | bytes 2339328 | tf_op jit(solution)/shard_map/while/body/jit(dynamic_update_index_in_dim)/dynamic_update_slice | solution.py:54
  34.9 5.8 %fusion.115 = bf16[4,4,16,128,128]{4,3,2,1,0:T(8,128)(2,1)} fusion(bf16[4,4,16,128,128]{4,3,2,1,0:T(8,128)(2,1)} %get-tuple-element.812, s32[]{:T(128)} %get-tuple-element.811, f32[4,16,128]{2,1,0:T(8,128)S(1)} %broadcast_select_fusion.11, f32[4,16,128]{2,1,0:T(8,128)S(1)} %bitcast.220, f32[4,16,128]{2,1,0:T(8,128)S(1)} %bitcast.219, ...), kind=kLoop, calls=%fused_computation.42.clone.1 | loop fusion | flops 29360128 | bytes 2339328 | tf_op jit(solution)/shard_map/while/body/jit(dynamic_update_index_in_dim)/dynamic_update_slice | solution.py:54
  44.4 5.8 %fusion.115 = bf16[4,4,16,128,128]{4,3,2,1,0:T(8,128)(2,1)} fusion(bf16[4,4,16,128,128]{4,3,2,1,0:T(8,128)(2,1)} %get-tuple-element.812, s32[]{:T(128)} %get-tuple-element.811, f32[4,16,128]{2,1,0:T(8,128)S(1)} %broadcast_select_fusion.11, f32[4,16,128]{2,1,0:T(8,128)S(1)} %bitcast.220, f32[4,16,128]{2,1,0:T(8,128)S(1)} %bitcast.219, ...), kind=kLoop, calls=%fused_computation.42.clone.1 | loop fusion | flops 29360128 | bytes 2339328 | tf_op jit(solution)/shard_map/while/body/jit(dynamic_update_index_in_dim)/dynamic_update_slice | solution.py:54
  53.9 5.9 %fusion.115 = bf16[4,4,16,128,128]{4,3,2,1,0:T(8,128)(2,1)} fusion(bf16[4,4,16,128,128]{4,3,2,1,0:T(8,128)(2,1)} %get-tuple-element.812, s32[]{:T(128)} %get-tuple-element.811, f32[4,16,128]{2,1,0:T(8,128)S(1)} %broadcast_select_fusion.11, f32[4,16,128]{2,1,0:T(8,128)S(1)} %bitcast.220, f32[4,16,128]{2,1,0:T(8,128)S(1)} %bitcast.219, ...), kind=kLoop, calls=%fused_computation.42.clone.1 | loop fusion | flops 29360128 | bytes 2339328 | tf_op jit(solution)/shard_map/while/body/jit(dynamic_update_index_in_dim)/dynamic_update_slice | solution.py:54
  60.0 14.0 %while.61 = (s32[]{:T(128)}, f32[4,4,75,128]{3,1,0,2:T(4,128)S(1)}, s32[4,4,16]{2,1,0:T(4,128)S(1)}, bf16[16,75,128]{2,1,0:T(8,128)(2,1)S(1)}, bf16[4,4,16,128,128]{4,3,2,1,0:T(8,128)(2,1)}, /*index=5*/s32[]{:T(128)}) while((s32[]{:T(128)}, f32[4,4,75,128]{3,1,0,2:T(4,128)S(1)}, s32[4,4,16]{2,1,0:T(4,128)S(1)}, ...), condition=%wide.region_3.6_spmd, body=%wide.region_2.5_spmd.sunk | while | flops 157902208 | bytes 6260941 | solution.py:68
  60.9 2.5 fusion.118
  64.4 2.5 fusion.118
  67.9 2.5 fusion.118
  71.4 2.5 fusion.118
  77.8 6.0 %all-to-all-start.4 = ((bf16[32,2,128]{2,1,0:T(2,128)(2,1)}), bf16[32,2,128]{2,1,0:T(2,128)(2,1)S(1)}, u32[]{:S(2)}, u32[]{:S(2)}) async-start(bf16[32,2,128]{2,1,0:T(2,128)(2,1)} %select_convert_fusion), calls=%async_computation.4 | async-start | bytes 32768 | tf_op jit(solution)/shard_map/all_to_all | solution.py:137
  84.7 5.4 %gather_fusion.13 = bf16[64,75,128]{2,0,1:T(8,128)(2,1)S(1)} fusion(bf16[16,75,128]{2,0,1:T(8,128)(2,1)S(1)} %copy-done.1, s32[1024]{0:T(1024)S(1)} %pad_clamp_fusion.7), kind=kCustom, calls=%fused_computation.4.clone | custom fusion | bytes 2457856 | tf_op jit(solution)/shard_map/jit(_take)/gather | solution.py:111
  90.8 5.0 %all-to-all-start.2 = ((bf16[32,2,3,128]{3,1,2,0:T(2,128)(2,1)}), bf16[32,2,3,128]{3,1,2,0:T(2,128)(2,1)S(1)}, u32[]{:S(2)}, u32[]{:S(2)}) async-start(bf16[32,2,3,128]{3,1,2,0:T(2,128)(2,1)} %get-tuple-element.493), calls=%async_computation.2 | async-start | bytes 98304 | tf_op jit(solution)/shard_map/all_to_all | solution.py:123
  95.8 2.5 broadcast_select_fusion.7
  98.3 4.7 %all-to-all-done.2 = bf16[32,2,3,128]{3,1,2,0:T(2,128)(2,1)S(1)} async-done(((bf16[32,2,3,128]{3,1,2,0:T(2,128)(2,1)}), bf16[32,2,3,128]{3,1,2,0:T(2,128)(2,1)S(1)}, u32[]{:S(2)}, u32[]{:S(2)}) %all-to-all-start.2) | async-done | bytes 49184 | tf_op jit(solution)/shard_map/all_to_all | solution.py:123
  103.0 2.6 all-to-all-start.3
  105.8 7.1 %all-to-all-done.3 = bf16[32,2,3,128]{3,1,2,0:T(2,128)(2,1)S(1)} async-done(((bf16[32,2,3,128]{3,1,2,0:T(2,128)(2,1)}), bf16[32,2,3,128]{3,1,2,0:T(2,128)(2,1)S(1)}, u32[]{:S(2)}, u32[]{:S(2)}) %all-to-all-start.3) | async-done | bytes 49184 | tf_op jit(solution)/shard_map/all_to_all | solution.py:130
  112.8 2.9 %all-to-all-start.1 = ((bf16[32,2,75,128]{3,1,2,0:T(2,128)(2,1)}), bf16[32,2,75,128]{3,1,2,0:T(2,128)(2,1)S(1)}, u32[]{:S(2)}, u32[]{:S(2)}) async-start(bf16[32,2,75,128]{3,1,2,0:T(2,128)(2,1)} %broadcast_select_fusion.7), calls=%async_computation.1 | async-start | bytes 2457600 | tf_op jit(solution)/shard_map/all_to_all | solution.py:122
  115.9 43.3 %while.62 = (s32[]{:T(128)}, bf16[4,4,24,128,128]{4,3,2,1,0:T(8,128)(2,1)}, s32[4]{0:T(128)S(1)}, f32[16,3,128]{2,0,1:T(8,128)S(1)}, s32[16,24]{1,0:T(8,128)S(1)...) while((s32[]{:T(128)}, ...), condition=%wide.region_9.14_spmd, body=%wide.region_8.13_spmd.sunk | while | flops 44127816 | bytes 5500943 | solution.py:54
  119.6 7.2 %fusion.119 = bf16[4,4,24,128,128]{4,3,2,1,0:T(8,128)(2,1)} fusion(bf16[4,4,24,128,128]{4,3,2,1,0:T(8,128)(2,1)} %get-tuple-element.871, s32[]{:T(128)} %get-tuple-element.870, f32[4,24,128]{2,1,0:T(8,128)S(1)} %broadcast_select_fusion.13, f32[4,24,128]{2,1,0:T(8,128)S(1)} %get-tuple-element.765, f32[4,24,128]{2,1,0:T(8,128)S(1)} %get-tuple-element.766, ...), kind=kLoop, calls=%fused_computation.92.clone.1 | loop fusion | flops 44040192 | bytes 3502592 | tf_op jit(solution)/shard_map/while/body/jit(dynamic_update_index_in_dim)/dynamic_update_slice | solution.py:54
  130.4 7.2 %fusion.119 = bf16[4,4,24,128,128]{4,3,2,1,0:T(8,128)(2,1)} fusion(bf16[4,4,24,128,128]{4,3,2,1,0:T(8,128)(2,1)} %get-tuple-element.871, s32[]{:T(128)} %get-tuple-element.870, f32[4,24,128]{2,1,0:T(8,128)S(1)} %broadcast_select_fusion.13, f32[4,24,128]{2,1,0:T(8,128)S(1)} %get-tuple-element.765, f32[4,24,128]{2,1,0:T(8,128)S(1)} %get-tuple-element.766, ...), kind=kLoop, calls=%fused_computation.92.clone.1 | loop fusion | flops 44040192 | bytes 3502592 | tf_op jit(solution)/shard_map/while/body/jit(dynamic_update_index_in_dim)/dynamic_update_slice | solution.py:54
  141.2 7.2 %fusion.119 = bf16[4,4,24,128,128]{4,3,2,1,0:T(8,128)(2,1)} fusion(bf16[4,4,24,128,128]{4,3,2,1,0:T(8,128)(2,1)} %get-tuple-element.871, s32[]{:T(128)} %get-tuple-element.870, f32[4,24,128]{2,1,0:T(8,128)S(1)} %broadcast_select_fusion.13, f32[4,24,128]{2,1,0:T(8,128)S(1)} %get-tuple-element.765, f32[4,24,128]{2,1,0:T(8,128)S(1)} %get-tuple-element.766, ...), kind=kLoop, calls=%fused_computation.92.clone.1 | loop fusion | flops 44040192 | bytes 3502592 | tf_op jit(solution)/shard_map/while/body/jit(dynamic_update_index_in_dim)/dynamic_update_slice | solution.py:54
  152.0 7.2 %fusion.119 = bf16[4,4,24,128,128]{4,3,2,1,0:T(8,128)(2,1)} fusion(bf16[4,4,24,128,128]{4,3,2,1,0:T(8,128)(2,1)} %get-tuple-element.871, s32[]{:T(128)} %get-tuple-element.870, f32[4,24,128]{2,1,0:T(8,128)S(1)} %broadcast_select_fusion.13, f32[4,24,128]{2,1,0:T(8,128)S(1)} %get-tuple-element.765, f32[4,24,128]{2,1,0:T(8,128)S(1)} %get-tuple-element.766, ...), kind=kLoop, calls=%fused_computation.92.clone.1 | loop fusion | flops 44040192 | bytes 3502592 | tf_op jit(solution)/shard_map/while/body/jit(dynamic_update_index_in_dim)/dynamic_update_slice | solution.py:54
  162.3 19.6 %while.63 = (s32[]{:T(128)}, f32[4,4,75,128]{3,1,0,2:T(4,128)}, s32[4,4,24]{2,1,0:T(4,128)S(1)}, bf16[64,75,128]{2,1,0:T(8,128)(2,1)S(1)}, bf16[4,4,24,128,128]{4,3,2,1,0:T(8,128)(2,1)}, /*index=5*/s32[]{:T(128)}) while((s32[]{:T(128)}, f32[4,4,75,128]{3,1,0,2:T(4,128)}, s32[4,4,24]{2,1,0:T(4,128)S(1)}, ...), condition=%wide.region_11.18_spmd, body=%wide.region_10.17_spmd.sunk | while | flops 236852800 | bytes 9143817 | solution.py:68
  163.3 3.1 %fusion.122 = f32[1,4,75,128]{3,2,1,0:T(8,128)S(1)} fusion(bf16[4,4,24,128,128]{4,3,2,1,0:T(8,128)(2,1)} %get-tuple-element.916, s32[]{:T(128)} %get-tuple-element.906, bf16[4,24,75,128]{3,2,1,0:T(8,128)(2,1)S(1)} %bitcast.201, pred[4,24]{1,0:T(4,128)(4,1)S(1)} %get-tuple-element.783), kind=kOutput, calls=%fused_computation.116.clone.1 | convolution fusion | flops 236851200 | bytes 5143136 | tf_op jit(solution)/shard_map/while/body/eval_jaxpr/wxmy,wxsy->wms/dot_general | solution.py:64
  168.2 3.1 %fusion.122 = f32[1,4,75,128]{3,2,1,0:T(8,128)S(1)} fusion(bf16[4,4,24,128,128]{4,3,2,1,0:T(8,128)(2,1)} %get-tuple-element.916, s32[]{:T(128)} %get-tuple-element.906, bf16[4,24,75,128]{3,2,1,0:T(8,128)(2,1)S(1)} %bitcast.201, pred[4,24]{1,0:T(4,128)(4,1)S(1)} %get-tuple-element.783), kind=kOutput, calls=%fused_computation.116.clone.1 | convolution fusion | flops 236851200 | bytes 5143136 | tf_op jit(solution)/shard_map/while/body/eval_jaxpr/wxmy,wxsy->wms/dot_general | solution.py:64
  173.1 3.1 %fusion.122 = f32[1,4,75,128]{3,2,1,0:T(8,128)S(1)} fusion(bf16[4,4,24,128,128]{4,3,2,1,0:T(8,128)(2,1)} %get-tuple-element.916, s32[]{:T(128)} %get-tuple-element.906, bf16[4,24,75,128]{3,2,1,0:T(8,128)(2,1)S(1)} %bitcast.201, pred[4,24]{1,0:T(4,128)(4,1)S(1)} %get-tuple-element.783), kind=kOutput, calls=%fused_computation.116.clone.1 | convolution fusion | flops 236851200 | bytes 5143136 | tf_op jit(solution)/shard_map/while/body/eval_jaxpr/wxmy,wxsy->wms/dot_general | solution.py:64
  178.1 3.1 %fusion.122 = f32[1,4,75,128]{3,2,1,0:T(8,128)S(1)} fusion(bf16[4,4,24,128,128]{4,3,2,1,0:T(8,128)(2,1)} %get-tuple-element.916, s32[]{:T(128)} %get-tuple-element.906, bf16[4,24,75,128]{3,2,1,0:T(8,128)(2,1)S(1)} %bitcast.201, pred[4,24]{1,0:T(4,128)(4,1)S(1)} %get-tuple-element.783), kind=kOutput, calls=%fused_computation.116.clone.1 | convolution fusion | flops 236851200 | bytes 5143136 | tf_op jit(solution)/shard_map/while/body/eval_jaxpr/wxmy,wxsy->wms/dot_general | solution.py:64
  186.9 2.6 broadcast_select_fusion.6
  189.4 5.9 %all-to-all-start.5 = ((bf16[32,2,75,128]{3,1,2,0:T(2,128)(2,1)}), bf16[32,2,75,128]{3,1,2,0:T(2,128)(2,1)S(1)}, u32[]{:S(2)}, u32[]{:S(2)}) async-start(bf16[32,2,75,128]{3,1,2,0:T(2,128)(2,1)} %broadcast_select_fusion.6), calls=%async_computation.5 | async-start | bytes 2457600 | tf_op jit(solution)/shard_map/all_to_all | solution.py:156
  195.4 16.7 %while.64 = (s32[]{:T(128)}, f32[4,4,75,128]{3,1,0,2:T(4,128)S(1)}, s32[4,4,16]{2,1,0:T(4,128)}, bf16[16,75,128]{2,1,0:T(8,128)(2,1)S(1)}, bf16[4,4,16,128,128]{4,3,2,1,0:T(8,128)(2,1)}, /*index=5*/s32[]{:T(128)}) while((s32[]{:T(128)}, f32[4,4,75,128]{3,1,0,2:T(4,128)S(1)}, s32[4,4,16]{2,1,0:T(4,128)}, ...), condition=%wide.region_13.20_spmd, body=%wide.region_12.19_spmd.sunk | while | flops 157902208 | bytes 6260941 | solution.py:68
  197.0 2.5 fusion.125
  201.2 2.5 fusion.125
  205.3 2.5 fusion.125
  209.5 2.5 fusion.125
  212.1 14.3 %all-to-all-done.5 = bf16[32,2,75,128]{3,1,2,0:T(2,128)(2,1)S(1)} async-done(((bf16[32,2,75,128]{3,1,2,0:T(2,128)(2,1)}), bf16[32,2,75,128]{3,1,2,0:T(2,128)(2,1)S(1)}, u32[]{:S(2)}, u32[]{:S(2)}) %all-to-all-start.5) | async-done | bytes 1228832 | tf_op jit(solution)/shard_map/all_to_all | solution.py:156
  229.5 19.6 %while.65 = (s32[]{:T(128)}, f32[4,4,75,128]{3,1,0,2:T(4,128)}, s32[4,4,24]{2,1,0:T(4,128)S(1)}, bf16[64,75,128]{2,1,0:T(8,128)(2,1)S(1)}, bf16[4,4,24,128,128]{4,3,2,1,0:T(8,128)(2,1)}, /*index=5*/s32[]{:T(128)}) while((s32[]{:T(128)}, f32[4,4,75,128]{3,1,0,2:T(4,128)}, s32[4,4,24]{2,1,0:T(4,128)S(1)}, ...), condition=%wide.region_15.22_spmd, body=%wide.region_14.21_spmd.sunk | while | flops 236852800 | bytes 9143817 | solution.py:68
  230.5 3.1 %fusion.128 = f32[1,4,75,128]{3,2,1,0:T(8,128)S(1)} fusion(bf16[4,4,24,128,128]{4,3,2,1,0:T(8,128)(2,1)} %get-tuple-element.952, s32[]{:T(128)} %get-tuple-element.942, bf16[4,24,75,128]{3,2,1,0:T(8,128)(2,1)S(1)} %bitcast.202, pred[4,24]{1,0:T(4,128)(4,1)S(1)} %get-tuple-element.797), kind=kOutput, calls=%fused_computation.142.clone.1 | convolution fusion | flops 236851200 | bytes 5143136 | tf_op jit(solution)/shard_map/while/body/eval_jaxpr/wxmy,wxsy->wms/dot_general | solution.py:64
  235.4 3.1 %fusion.128 = f32[1,4,75,128]{3,2,1,0:T(8,128)S(1)} fusion(bf16[4,4,24,128,128]{4,3,2,1,0:T(8,128)(2,1)} %get-tuple-element.952, s32[]{:T(128)} %get-tuple-element.942, bf16[4,24,75,128]{3,2,1,0:T(8,128)(2,1)S(1)} %bitcast.202, pred[4,24]{1,0:T(4,128)(4,1)S(1)} %get-tuple-element.797), kind=kOutput, calls=%fused_computation.142.clone.1 | convolution fusion | flops 236851200 | bytes 5143136 | tf_op jit(solution)/shard_map/while/body/eval_jaxpr/wxmy,wxsy->wms/dot_general | solution.py:64
  240.3 3.1 %fusion.128 = f32[1,4,75,128]{3,2,1,0:T(8,128)S(1)} fusion(bf16[4,4,24,128,128]{4,3,2,1,0:T(8,128)(2,1)} %get-tuple-element.952, s32[]{:T(128)} %get-tuple-element.942, bf16[4,24,75,128]{3,2,1,0:T(8,128)(2,1)S(1)} %bitcast.202, pred[4,24]{1,0:T(4,128)(4,1)S(1)} %get-tuple-element.797), kind=kOutput, calls=%fused_computation.142.clone.1 | convolution fusion | flops 236851200 | bytes 5143136 | tf_op jit(solution)/shard_map/while/body/eval_jaxpr/wxmy,wxsy->wms/dot_general | solution.py:64
  245.2 3.1 %fusion.128 = f32[1,4,75,128]{3,2,1,0:T(8,128)S(1)} fusion(bf16[4,4,24,128,128]{4,3,2,1,0:T(8,128)(2,1)} %get-tuple-element.952, s32[]{:T(128)} %get-tuple-element.942, bf16[4,24,75,128]{3,2,1,0:T(8,128)(2,1)S(1)} %bitcast.202, pred[4,24]{1,0:T(4,128)(4,1)S(1)} %get-tuple-element.797), kind=kOutput, calls=%fused_computation.142.clone.1 | convolution fusion | flops 236851200 | bytes 5143136 | tf_op jit(solution)/shard_map/while/body/eval_jaxpr/wxmy,wxsy->wms/dot_general | solution.py:64
  249.0 2.7 fusion.83
  252.5 19.1 %all-reduce = (f32[]{:T(128)}, f32[]{:T(128)}) all-reduce(f32[]{:T(128)} %get-tuple-element.360, f32[]{:T(128)} %get-tuple-element.359), channel_id=1, replica_groups=mesh['gx'=4,'gy'=8] {'gy'}, use_global_device_ids=true, to_apply=%region_20.27 | all-reduce | flops 2 | bytes 16 | tf_op jit(solution)/shard_map/psum | solution.py:79
  271.6 6.5 %all-reduce.1 = (f32[1]{0:T(128)}, f32[1]{0:T(128)}) all-reduce(f32[1]{0:T(128)} %bitcast.78, f32[1]{0:T(128)} %bitcast.77), channel_id=1, replica_groups=mesh['gx'=4,'gy'=8] {'gx'}, use_global_device_ids=true, to_apply=%region_21.28 | all-reduce | flops 2 | bytes 16 | tf_op jit(solution)/shard_map/psum | solution.py:79
  (267 shorter events, 70.5 us)
Async XLA Ops:
  0.6 0.8 copy-start
  1.5 4.4 %copy-start.11 = (s32[16,40]{1,0:T(8,128)S(1)}, s32[16,40]{1,0:T(8,128)}, u32[]{:S(2)}) copy-start(s32[16,40]{1,0:T(8,128)} %param.36) | copy-start | bytes 7684
  11.2 62.9 %all-to-all-start = ((s32[32,1,2]{2,1,0:T(1,128)}), s32[32,1,2]{2,1,0:T(1,128)S(1)}, u32[]{:S(2)}, u32[]{:S(2)}) async-start(s32[32,1,2]{2,1,0:T(1,128)} %copy.220), calls=%async_computation | async-start | bytes 32768 | tf_op jit(solution)/shard_map/all_to_all | solution.py:104
  18.7 3.0 %copy-start.3 = (f32[16,3,128]{2,0,1:T(8,128)S(1)}, f32[16,3,128]{2,0,1:T(8,128)}, u32[]{:S(2)}) copy-start(f32[16,3,128]{2,0,1:T(8,128)} %param.33) | copy-start | bytes 73732
  18.7 3.0 %copy-start.4 = (f32[16,3,128]{2,0,1:T(8,128)S(1)}, f32[16,3,128]{2,0,1:T(8,128)}, u32[]{:S(2)}) copy-start(f32[16,3,128]{2,0,1:T(8,128)} %param.32) | copy-start | bytes 73732
  18.7 3.0 %copy-start.2 = (f32[16,128]{1,0:T(8,128)S(1)}, f32[16,128]{1,0:T(8,128)}, u32[]{:S(2)}) copy-start(f32[16,128]{1,0:T(8,128)} %param.34) | copy-start | bytes 24580
  21.7 38.0 %copy-start.1 = (bf16[16,75,128]{2,0,1:T(8,128)(2,1)S(1)}, bf16[16,75,128]{2,0,1:T(8,128)(2,1)}, u32[]{:S(2)}) copy-start(bf16[16,75,128]{2,0,1:T(8,128)(2,1)} %param.31) | copy-start | bytes 921604
  74.0 0.6 copy-start.9
  74.0 16.1 %copy-start.7 = (f32[4,4,75,128]{3,1,0,2:T(4,128)}, f32[4,4,75,128]{3,1,0,2:T(4,128)S(1)}, u32[]{:S(2)}) copy-start(f32[4,4,75,128]{3,1,0,2:T(4,128)S(1)} %get-tuple-element.202) | copy-start | bytes 1843204
  77.8 13.0 %all-to-all-start.4 = ((bf16[32,2,128]{2,1,0:T(2,128)(2,1)}), bf16[32,2,128]{2,1,0:T(2,128)(2,1)S(1)}, u32[]{:S(2)}, u32[]{:S(2)}) async-start(bf16[32,2,128]{2,1,0:T(2,128)(2,1)} %select_convert_fusion), calls=%async_computation.4 | async-start | bytes 32768 | tf_op jit(solution)/shard_map/all_to_all | solution.py:137
  90.8 12.2 %all-to-all-start.2 = ((bf16[32,2,3,128]{3,1,2,0:T(2,128)(2,1)}), bf16[32,2,3,128]{3,1,2,0:T(2,128)(2,1)S(1)}, u32[]{:S(2)}, u32[]{:S(2)}) async-start(bf16[32,2,3,128]{3,1,2,0:T(2,128)(2,1)} %get-tuple-element.493), calls=%async_computation.2 | async-start | bytes 98304 | tf_op jit(solution)/shard_map/all_to_all | solution.py:123
  103.0 9.8 %all-to-all-start.3 = ((bf16[32,2,3,128]{3,1,2,0:T(2,128)(2,1)}), bf16[32,2,3,128]{3,1,2,0:T(2,128)(2,1)S(1)}, u32[]{:S(2)}, u32[]{:S(2)}) async-start(bf16[32,2,3,128]{3,1,2,0:T(2,128)(2,1)} %get-tuple-element.492), calls=%async_computation.3 | async-start | bytes 98304 | tf_op jit(solution)/shard_map/all_to_all | solution.py:130
  112.8 46.4 %all-to-all-start.1 = ((bf16[32,2,75,128]{3,1,2,0:T(2,128)(2,1)}), bf16[32,2,75,128]{3,1,2,0:T(2,128)(2,1)S(1)}, u32[]{:S(2)}, u32[]{:S(2)}) async-start(bf16[32,2,75,128]{3,1,2,0:T(2,128)(2,1)} %broadcast_select_fusion.7), calls=%async_computation.1 | async-start | bytes 2457600 | tf_op jit(solution)/shard_map/all_to_all | solution.py:122
  162.3 21.3 %copy-start.10 = (f32[16,3,128]{2,0,1:T(8,128)S(1)}, f32[16,3,128]{2,0,1:T(8,128)}, u32[]{:S(2)}) copy-start(f32[16,3,128]{2,0,1:T(8,128)} %param.35) | copy-start | bytes 73732
  183.4 0.8 copy-start.5
  184.2 0.8 copy-start.6
  189.4 37.0 %all-to-all-start.5 = ((bf16[32,2,75,128]{3,1,2,0:T(2,128)(2,1)}), bf16[32,2,75,128]{3,1,2,0:T(2,128)(2,1)S(1)}, u32[]{:S(2)}, u32[]{:S(2)}) async-start(bf16[32,2,75,128]{3,1,2,0:T(2,128)(2,1)} %broadcast_select_fusion.6), calls=%async_computation.5 | async-start | bytes 2457600 | tf_op jit(solution)/shard_map/all_to_all | solution.py:156
  212.1 17.4 %copy-start.8 = (f32[4,4,75,128]{3,1,0,2:T(4,128)}, f32[4,4,75,128]{3,1,0,2:T(4,128)S(1)}, u32[]{:S(2)}) copy-start(f32[4,4,75,128]{3,1,0,2:T(4,128)S(1)} %get-tuple-element.205) | copy-start | bytes 1843204
